TPU v7x, 256 devices: a whole 4x4x8 slice. The times are simulated.
256 devices in a mesh: row: 32 (over z, x), col: 8 (over y, core).
Axes of the slice: x: 4, y: 4, z: 8, core: 2. Of those that a mesh axis runs over, the one named last changes fastest.
Arguments:
- integrals: bfloat16 [65536, 8192], P('row', 'col'), may hold values from -0.0234375 to 0.0234375
- lambda2: bfloat16 [2016, 65536], P('col', 'row'), may hold values from -6 to 6
- source_terms: float32 [2016, 8192], P('row', 'col'), may hold values from -6 to 6
- hist_amp: bfloat16 [5, 2016, 8192], P(None, 'row', 'col'), may hold values from -6 to 6
- hist_err: bfloat16 [5, 2016, 8192], P(None, 'row', 'col'), may hold values from -64 to 64
- eps_occ: float32 [64], replicated, may hold values from -1 to -0.3
- eps_vir: float32 [800], replicated, may hold values from 0.1 to 1
- occ_pair: int32 [2, 2016], P(None, 'row'), may hold values from 0 to 63, as said below
- vir_pair: int32 [2, 8192], P(None, 'col'), may hold values from 0 to 799, as said below
Outputs:
- updated: float32 [2016, 8192], P('row', 'col')
Inputs may be any that keep to these rules, and one draw needn't show every extreme that they name: `occ_pair`: every pair i < j of the 64 occupied orbitals appears exactly once, in some order. `vir_pair`: in every column the first orbital is smaller than the second.
All inputs are finite; a program needn't handle non-finite values.
Results may differ from a plain program's by a relative error of at most 0.0003.
Values may be sent and summed in bfloat16 or wider, within the bound.
A program may use at most 64 MiB of HBM per device.

v0:
```python
import jax
import jax.numpy as jnp
from jax import lax
from jax.sharding import PartitionSpec as P

precise = lax.Precision.HIGHEST


def pair_energy(pairs, energies):
    levels = jnp.arange(energies.shape[0], dtype=jnp.int32)
    first = jnp.sum(jnp.where(pairs[0][:, None] == levels[None, :], energies[None, :], 0.0), axis=1)
    second = jnp.sum(
        jnp.where(pairs[1][:, None] == levels[None, :], energies[None, :], 0.0), axis=1
    )
    return first + second


def diis_weights(correlation):
    factor = jnp.linalg.cholesky(correlation)
    order = correlation.shape[0]
    forward = []
    for k in range(order):
        running = jnp.ones((), correlation.dtype)
        for m in range(k):
            running = running - factor[k, m] * forward[m]
        forward.append(running / factor[k, k])
    backward = [None] * order
    for k in reversed(range(order)):
        running = forward[k]
        for m in range(k + 1, order):
            running = running - factor[m, k] * backward[m]
        backward[k] = running / factor[k, k]
    solved = jnp.stack(backward)
    return solved / jnp.sum(solved)


def on_device(
    integrals, lambda2, source_terms, hist_amp, hist_err, eps_occ, eps_vir, occ_pair, vir_pair
):
    stored_count = hist_err.shape[0]
    flat_stored = hist_err.astype(jnp.float32).reshape(stored_count, -1)
    all_cols = lax.all_gather(lambda2, "col", axis=0, tiled=True)
    ladder = lax.psum_scatter(
        jnp.dot(all_cols, integrals, preferred_element_type=jnp.float32),
        "row",
        scatter_dimension=0,
        tiled=True,
    )
    denominator = pair_energy(occ_pair, eps_occ)[:, None] - pair_energy(vir_pair, eps_vir)[None, :]
    raw_update = (source_terms + ladder) / denominator
    err_new = raw_update - hist_amp[0].astype(jnp.float32)
    flat_new = err_new.reshape(1, -1)
    stacked = jnp.concatenate([flat_stored, flat_new], axis=0)
    correlation = lax.psum(jnp.dot(stacked, stacked.T, precision=precise), ("row", "col"))
    weights = diis_weights(correlation)
    updated = weights[stored_count] * raw_update
    for k in range(stored_count):
        updated = updated + weights[k] * hist_amp[k].astype(jnp.float32)
    return updated


def solution(mesh):
    placed = (
        P("row", "col"),
        P("col", "row"),
        P("row", "col"),
        P(None, "row", "col"),
        P(None, "row", "col"),
        P(),
        P(),
        P(None, "row"),
        P(None, "col"),
    )
    return jax.shard_map(
        on_device, mesh=mesh, in_specs=placed, out_specs=P("row", "col"), check_vma=False
    )
```

profile of v0, /device:TPU:1, one launch (start us, length us, event | category | flops | bytes accessed | tf_op | source)
XLA Modules:
  0.0 320.9 jit_solution(15406420744793112163)
XLA Ops:
  6.5 0.0 all-gather.3.cloned.1.call-start
  6.5 0.7 all-gather.3.cloned.1.call-update
  7.3 0.8 fusion.14
  8.0 1.5 select_reduce_fusion
  9.6 1.2 convert_bitcast_fusion
  10.8 54.8 %all-gather.3.cloned.1.call-done = bf16[8,252,2048]{2,1,0:T(8,128)(2,1)} async-done(((bf16[1,252,2048]{2,1,0:T(8,128)(2,1)}), bf16[8,252,2048]{2,1,0:T(8,128)(2,1)}) %all-gather.3.cloned.1.call-update) | async-done | bytes 8257552 | tf_op jit(solution)/shard_map/all_gather | solution.py:42
  65.7 7.5 %reshape.68 = bf16[2016,2048]{1,0:T(8,128)(2,1)} reshape(bf16[8,252,2048]{2,1,0:T(8,128)(2,1)} %all-gather.3.cloned.1.call-done) | data formatting | bytes 16515072
  73.1 14.2 %fusion.18 = f32[2016,1024]{1,0:T(8,128)} fusion(bf16[2016,2048]{1,0:T(8,128)(2,1)} %reshape.68, bf16[2048,1024]{1,0:T(8,128)(2,1)} %param.9), kind=kOutput, calls=%fused_computation.38 | convolution fusion | flops 8455716864 | bytes 20709376 | tf_op jit(solution)/shard_map/dot_general | solution.py:44
  87.4 0.0 copy-start.3
  87.4 100.2 %fusion = f32[64,1024]{1,0:T(8,128)S(1)} fusion(f32[2016,1024]{1,0:T(8,128)} %fusion.18), kind=kCustom, calls=%all-reduce-scatter | all-reduce-scatter fusion | flops 2097153 | bytes 8520704
  187.6 0.0 copy-start
  187.6 0.0 copy-start.5
  187.6 0.0 copy-start.4
  187.6 2.3 collective-permute-start
  189.9 0.0 copy-done.3
  190.0 0.0 copy-done
  190.0 0.8 copy.19
  190.8 0.0 copy-done.5
  190.8 0.0 copy-start.1
  190.8 0.0 copy-start.2
  190.8 0.6 dynamic-slice.4
  191.9 0.0 copy-done.4
  192.0 0.2 select_reduce_fusion.2
  192.2 0.0 collective-permute-done
  192.2 2.0 concatenate.4
  194.2 1.1 fusion.5
  195.3 0.3 copy.20
  195.6 4.5 %fusion.1 = f32[6,6]{0,1:T(8,128)S(1)} fusion(f32[1,64512]{1,0:T(1,128)S(1)} %bitcast.70, f32[5,64512]{1,0:T(8,128)S(1)} %bitcast.68), kind=kOutput, calls=%fused_computation.4 | convolution fusion | flops 28256256 | bytes 1548432 | tf_op jit(solution)/shard_map/dot_general | solution.py:54
  200.1 78.7 %psum.7 = f32[6,6]{0,1:T(8,128)S(1)} all-reduce(f32[6,6]{0,1:T(8,128)S(1)} %fusion.1), channel_id=1, replica_groups=mesh['row'=32,'col'=8] {'row','col'}, use_global_device_ids=true, to_apply=%region_5.6 | all-reduce | flops 36 | bytes 288 | tf_op jit(solution)/shard_map/psum | solution.py:54
  278.8 0.1 copy.17
  278.9 0.5 cholesky.18
  279.4 0.6 compare_reduce_fusion
  280.1 0.6 select_select_fusion
  280.7 0.6 fusion.16
  281.3 0.7 fusion.15
  308.7 0.1 stack.27
  308.7 0.7 fusion.17
  309.4 0.0 copy-done.1
  309.4 0.0 copy-done.2
  309.4 4.6 %fusion.10 = f32[63,1024]{1,0:T(8,128)} fusion(bf16[5,63,1024]{2,1,0:T(8,128)(2,1)S(1)} %copy-done.2, f32[]{:T(128)} %bitcast.43, f32[]{:T(128)} %bitcast.41, f32[]{:T(128)} %bitcast.39, f32[]{:T(128)} %bitcast.37, f32[]{:T(128)} %bitcast.35, f32[]{:T(128)} %bitcast.34, f32[1024]{0:T(1024)S(1)} %add.47, f32[63]{0:T(128)S(1)} %add.46, ...), kind=kLoop, calls=%fused_computation.16 | loop fusion | flops 1225728 | bytes 1423640 | tf_op jit(solution)/shard_map/add | solution.py:58
  (7 shorter events, 0.1 us)
Async XLA Ops:
  6.5 59.1 %all-gather.3.cloned.1.call-start = ((), (), s32[]{:S(2)}) async-start(), calls=%async_computation | async-start | bytes 9437184 | tf_op jit(solution)/shard_map/all_gather | solution.py:42
  87.4 102.6 %copy-start.3 = (s32[2,63]{1,0:T(2,128)S(1)}, s32[2,63]{1,0:T(2,128)}, u32[]{:S(2)}) copy-start(s32[2,63]{1,0:T(2,128)} %param.16) | copy-start | bytes 1516
  187.6 2.4 copy-start
  187.6 3.2 copy-start.5
  187.6 4.3 %copy-start.4 = (f32[64]{0:T(128)S(1)}, f32[64]{0:T(128)}, u32[]{:S(2)}) copy-start(f32[64]{0:T(128)} %param.14) | copy-start | bytes 772
  187.6 4.5 %collective-permute-start = (f32[31,1024]{1,0:T(8,128)S(1)}, f32[31,1024]{1,0:T(8,128)}, u32[]{:S(2)}, u32[]{:S(2)}) collective-permute-start(f32[31,1024]{1,0:T(8,128)S(1)} %slice.172), channel_id=1, source_target_pairs={{0,8},{8,16},{16,24},{24,32},{32,40},{40,48},{48,56},{56,64},{64,7... | collective-permute-start | bytes 380936
  190.8 118.6 %copy-start.1 = (f32[63,1024]{1,0:T(8,128)S(1)}, f32[63,1024]{1,0:T(8,128)}, u32[]{:S(2)}) copy-start(f32[63,1024]{1,0:T(8,128)} %param.11) | copy-start | bytes 774148
  190.8 118.6 %copy-start.2 = (bf16[5,63,1024]{2,1,0:T(8,128)(2,1)S(1)}, bf16[5,63,1024]{2,1,0:T(8,128)(2,1)}, u32[]{:S(2)}) copy-start(bf16[5,63,1024]{2,1,0:T(8,128)(2,1)} %param.12) | copy-start | bytes 1935364
Sparse Core Ops, SparseCore 0:
  9.2 56.4 all-gather.2
where the time goes:
time: 322 us; the launch traced here: 321 us
  blocking collectives  179 us (56%)
  waiting for transfers between devices  55.6 us (17%)
  between operations  40.7 us (13%)
  matrix products  18.7 us (6%)
  local copies, waits for them, and re-layouts  14.1 us (4%)
  other arithmetic  10.6 us (3%)
    unnamed x1, blocking collectives  100 us
    psum x1, blocking collectives, on_device(): lax.psum(jnp.dot(stacked, stacked.T, precision=precise), ('row', 'col'))  78.7 us
    all_gather x1, waiting for transfers between devices, on_device(): all_cols = lax.all_gather(lambda2, 'col', axis=0, tiled=True)  54.8 us
    dot_general x1, matrix products, on_device(): jnp.dot(all_cols, integrals, preferred_element_type=jnp.float32)  14.2 us
    unnamed x18, local copies, waits for them, and re-layouts  11.2 us
  transfers between devices with their start and end apart: 2, of which 1 were waited for; matrix products, arithmetic and copies ran while one was open for 2% of the time, Pallas kernels for 0%

commit v1 on v0

--- a/solution.py
+++ b/solution.py
@@ -51,7 +51,9 @@
     err_new = raw_update - hist_amp[0].astype(jnp.float32)
     flat_new = err_new.reshape(1, -1)
     stacked = jnp.concatenate([flat_stored, flat_new], axis=0)
-    correlation = lax.psum(jnp.dot(stacked, stacked.T, precision=precise), ("row", "col"))
+    x = jnp.dot(stacked, stacked.T, precision=precise)
+    parts = lax.all_gather(x, ("row", "col"))
+    correlation = jnp.sum(parts, axis=0)
     weights = diis_weights(correlation)
     updated = weights[stored_count] * raw_update
     for k in range(stored_count):

time: 322 us -> 310 us (0.963)
  blocking collectives: 179 us -> 167 us
    psum x1 -> x0, blocking collectives: 78.7 us -> none  [on_device(): lax.psum(jnp.dot(stacked, stacked.T, precision=precise), ('row', 'col'))]
    all_gather x0 -> x1, blocking collectives: none -> 66.5 us  [on_device(): parts = lax.all_gather(x, ('row', 'col'))]
where the time goes in v1:
time: 310 us; the launch traced here: 309 us
  blocking collectives  167 us (54%)
  waiting for transfers between devices  55.6 us (18%)
  between operations  40.7 us (13%)
  matrix products  18.9 us (6%)
  local copies, waits for them, and re-layouts  14.1 us (5%)
  other arithmetic  11 us (4%)
    unnamed x1, blocking collectives  100 us
    all_gather x1, blocking collectives, on_device(): parts = lax.all_gather(x, ('row', 'col'))  66.5 us
    all_gather x1, waiting for transfers between devices, on_device(): all_cols = lax.all_gather(lambda2, 'col', axis=0, tiled=True)  54.8 us
    dot_general x1, matrix products, on_device(): jnp.dot(all_cols, integrals, preferred_element_type=jnp.float32)  14.2 us
    unnamed x18, local copies, waits for them, and re-layouts  11.2 us
  transfers between devices with their start and end apart: 2, of which 1 were waited for; matrix products, arithmetic and copies ran while one was open for 2% of the time, Pallas kernels for 0%

profile of v1, /device:TPU:1, one launch (start us, length us, event | category | flops | bytes accessed | tf_op | source)
XLA Modules:
  0.0 309.3 jit_solution(8957906457682440149)
XLA Ops:
  6.5 0.0 all-gather.5.cloned.1.call-start
  6.5 0.7 all-gather.5.cloned.1.call-update
  7.3 0.8 fusion.17
  8.0 1.5 select_reduce_fusion
  9.6 1.2 convert_bitcast_fusion
  10.8 54.8 %all-gather.5.cloned.1.call-done = bf16[8,252,2048]{2,1,0:T(8,128)(2,1)} async-done(((bf16[1,252,2048]{2,1,0:T(8,128)(2,1)}), bf16[8,252,2048]{2,1,0:T(8,128)(2,1)}) %all-gather.5.cloned.1.call-update) | async-done | bytes 8257552 | tf_op jit(solution)/shard_map/all_gather | solution.py:42
  65.7 7.5 %reshape.69 = bf16[2016,2048]{1,0:T(8,128)(2,1)} reshape(bf16[8,252,2048]{2,1,0:T(8,128)(2,1)} %all-gather.5.cloned.1.call-done) | data formatting | bytes 16515072
  73.1 14.2 %fusion.21 = f32[2016,1024]{1,0:T(8,128)} fusion(bf16[2016,2048]{1,0:T(8,128)(2,1)} %reshape.69, bf16[2048,1024]{1,0:T(8,128)(2,1)} %param.9), kind=kOutput, calls=%fused_computation.39 | convolution fusion | flops 8455716864 | bytes 20709376 | tf_op jit(solution)/shard_map/dot_general | solution.py:44
  87.4 0.0 copy-start.3
  87.4 100.2 %fusion = f32[64,1024]{1,0:T(8,128)S(1)} fusion(f32[2016,1024]{1,0:T(8,128)} %fusion.21), kind=kCustom, calls=%all-reduce-scatter | all-reduce-scatter fusion | flops 2097153 | bytes 8520704
  187.6 0.0 copy-start
  187.6 0.0 copy-start.5
  187.6 0.0 copy-start.4
  187.6 2.3 collective-permute-start
  190.0 0.0 copy-done.3
  190.0 0.0 copy-done
  190.0 0.8 copy.14
  190.8 0.0 copy-done.5
  190.8 0.6 dynamic-slice.4
  191.9 0.0 copy-done.4
  191.9 0.2 select_reduce_fusion.2
  192.2 0.0 collective-permute-done
  192.2 2.0 concatenate.4
  194.2 0.0 copy-start.1
  194.2 0.0 copy-start.2
  194.2 1.2 fusion.8
  195.4 0.3 copy.15
  195.7 4.7 %fusion.5 = f32[1,6,6]{2,1,0:T(8,128)S(1)} fusion(f32[1,64512]{1,0:T(1,128)S(1)} %bitcast.72, f32[5,64512]{1,0:T(8,128)S(1)} %bitcast.70), kind=kOutput, calls=%fused_computation.9 | convolution fusion | flops 28256256 | bytes 1548432 | tf_op jit(solution)/shard_map/dot_general | solution.py:54
  200.3 66.5 %all-gather.2 = f32[256,6,6]{2,1,0:T(8,128)S(1)} all-gather(f32[1,6,6]{2,1,0:T(8,128)S(1)} %fusion.5), channel_id=2, replica_groups=mesh['row'=32,'col'=8] {'row','col'}, dimensions={0}, use_global_device_ids=true | all-gather | bytes 37008 | tf_op jit(solution)/shard_map/all_gather | solution.py:55
  266.8 0.3 reduce_sum.68
  267.1 0.1 copy.13
  267.2 0.5 cholesky.18
  267.8 0.6 compare_reduce_fusion
  268.4 0.6 select_select_fusion
  269.1 0.6 fusion.19
  269.7 0.7 fusion.18
  297.0 0.1 stack.27
  297.1 0.7 fusion.20
  297.8 0.0 copy-done.1
  297.8 0.0 copy-done.2
  297.8 4.6 %fusion.13 = f32[63,1024]{1,0:T(8,128)} fusion(bf16[5,63,1024]{2,1,0:T(8,128)(2,1)S(1)} %copy-done.2, f32[]{:T(128)} %bitcast.44, f32[]{:T(128)} %bitcast.42, f32[]{:T(128)} %bitcast.40, f32[]{:T(128)} %bitcast.38, f32[]{:T(128)} %bitcast.36, f32[]{:T(128)} %bitcast.35, f32[1024]{0:T(1024)S(1)} %add.45, f32[63]{0:T(128)S(1)} %add.44, ...), kind=kLoop, calls=%fused_computation.17 | loop fusion | flops 1225728 | bytes 1423640 | tf_op jit(solution)/shard_map/add | solution.py:60
  (7 shorter events, 0.1 us)
Async XLA Ops:
  6.5 59.1 %all-gather.5.cloned.1.call-start = ((), (), s32[]{:S(2)}) async-start(), calls=%async_computation | async-start | bytes 9437184 | tf_op jit(solution)/shard_map/all_gather | solution.py:42
  87.4 102.6 %copy-start.3 = (s32[2,63]{1,0:T(2,128)S(1)}, s32[2,63]{1,0:T(2,128)}, u32[]{:S(2)}) copy-start(s32[2,63]{1,0:T(2,128)} %param.16) | copy-start | bytes 1516
  187.6 2.4 copy-start
  187.6 3.2 %copy-start.5 = (u32[256]{0:T(256)S(1)}, u32[256]{0:T(256)}, u32[]{:S(2)}) copy-start(u32[256]{0:T(256)} %constant.47) | copy-start | bytes 3076
  187.6 4.3 %copy-start.4 = (f32[64]{0:T(128)S(1)}, f32[64]{0:T(128)}, u32[]{:S(2)}) copy-start(f32[64]{0:T(128)} %param.14) | copy-start | bytes 772
  187.6 4.5 %collective-permute-start = (f32[31,1024]{1,0:T(8,128)S(1)}, f32[31,1024]{1,0:T(8,128)}, u32[]{:S(2)}, u32[]{:S(2)}) collective-permute-start(f32[31,1024]{1,0:T(8,128)S(1)} %slice.172), channel_id=1, source_target_pairs={{0,8},{8,16},{16,24},{24,32},{32,40},{40,48},{48,56},{56,64},{64,7... | collective-permute-start | bytes 380936
  194.2 103.6 %copy-start.1 = (f32[63,1024]{1,0:T(8,128)S(1)}, f32[63,1024]{1,0:T(8,128)}, u32[]{:S(2)}) copy-start(f32[63,1024]{1,0:T(8,128)} %param.11) | copy-start | bytes 774148
  194.2 103.6 %copy-start.2 = (bf16[5,63,1024]{2,1,0:T(8,128)(2,1)S(1)}, bf16[5,63,1024]{2,1,0:T(8,128)(2,1)}, u32[]{:S(2)}) copy-start(bf16[5,63,1024]{2,1,0:T(8,128)(2,1)} %param.12) | copy-start | bytes 1935364
Sparse Core Ops, SparseCore 0:
  9.2 56.4 all-gather.4
